TPU v7x, 32 devices: a whole 2x2x4 slice. The times are simulated.
32 devices in a mesh: dp: 8 (over z, x), mp: 4 (over y, core).
Axes of the slice: x: 2, y: 2, z: 4, core: 2. Of those that a mesh axis runs over, the one named last changes fastest.
Arguments:
- teacher_states: bfloat16 [512, 128, 4096], P('dp', None, 'mp'), may hold values from -6 to 6
- teacher_gain: float32 [4096], P('mp'), may hold values from 0.25 to 1.75
- teacher_proj: bfloat16 [4096, 1024], P('mp'), may hold values from -0.09375 to 0.09375
- teacher_mask: int32 [512, 128], P('dp'), may hold values 0 or 1
- student_states: bfloat16 [1024, 64, 768], P(('dp', 'mp')), may hold values from -6 to 6
- student_gain: float32 [768], replicated, may hold values from 0.25 to 1.75
- student_proj: bfloat16 [768, 1024], replicated, may hold values from -0.21875 to 0.21875
- student_mask: int32 [1024, 64], P(('dp', 'mp')), may hold values 0 or 1
- positive: int32 [1024], P(('dp', 'mp')), may hold values from 0 to 511
Outputs:
- grad_embed: float32 [1024, 1024], P(('dp', 'mp'))
- grad_states: bfloat16 [1024, 64, 768], P(('dp', 'mp'))
All inputs are finite; a program needn't handle non-finite values. No bound on the sum of `teacher_mask` or of `student_mask` on one device may be relied on, other than what follows from the above.
Results may differ from a plain program's by a relative error of at most 0.0085.
Values may be sent and summed in bfloat16 or wider, within the bound.
A program may use at most 128 MiB of HBM per device.

v0:
```python
import jax
import jax.numpy as jnp
from jax import lax
from jax.sharding import PartitionSpec as P

D = 4096


def unit_rows(values):
    return (
        values
        * lax.rsqrt(jnp.mean(values * values, axis=-1, keepdims=True) + 1e-06)
        / jnp.sqrt(jnp.float32(values.shape[-1]))
    )


def student_forward(states, gain, proj, live_mask):
    values = states.astype(jnp.float32)
    scale = lax.rsqrt(jnp.mean(values * values, axis=-1, keepdims=True) + 1e-06)
    normed = (values * scale * gain).astype(jnp.bfloat16)
    flat = normed.reshape(-1, normed.shape[-1])
    act = jax.nn.gelu(jnp.dot(flat, proj, preferred_element_type=jnp.float32), approximate=True)
    act = act.reshape(states.shape[0], states.shape[1], -1)
    live = live_mask.astype(jnp.float32)
    pooled = jnp.sum(act * live[:, :, None], axis=1)
    return unit_rows(pooled)


def shards(
    teacher_states,
    teacher_gain,
    teacher_proj,
    teacher_mask,
    student_states,
    student_gain,
    student_proj,
    student_mask,
    positive,
):
    values = teacher_states.astype(jnp.float32)
    partial_squares = jnp.sum(values * values, axis=-1)
    squares = lax.psum(partial_squares, "mp")
    scale = lax.rsqrt(squares / D + 1e-06)
    live = teacher_mask.astype(jnp.float32)
    weight = live * scale
    pooled = jnp.sum(values * weight[:, :, None], axis=1)
    tpooled = (pooled * teacher_gain).astype(jnp.bfloat16)
    partial_embed = jnp.dot(tpooled, teacher_proj, preferred_element_type=jnp.float32)
    summed = lax.psum(partial_embed, "mp")
    group_emb = unit_rows(summed).astype(jnp.bfloat16)
    gathered = lax.all_gather(group_emb, "dp", axis=0, tiled=True)
    semb, back = jax.vjp(
        lambda st: student_forward(st, student_gain, student_proj, student_mask), student_states
    )
    sround = semb.astype(jnp.bfloat16)
    columns = lax.broadcasted_iota(jnp.int32, (positive.shape[0], gathered.shape[0]), 1)
    picker = (positive[:, None] == columns).astype(jnp.bfloat16)
    tpos = jnp.dot(picker, gathered, preferred_element_type=jnp.float32).astype(jnp.bfloat16)
    tlogit = 10.0 * jnp.dot(tpos, gathered.T, preferred_element_type=jnp.float32)
    slogit = 20.0 * jnp.dot(sround, gathered.T, preferred_element_type=jnp.float32)
    texp = jnp.exp(tlogit)
    sexp = jnp.exp(slogit)
    diff = (
        sexp / jnp.sum(sexp, axis=1, keepdims=True) - texp / jnp.sum(texp, axis=1, keepdims=True)
    ).astype(jnp.bfloat16)
    grad_embed = 20.0 * jnp.dot(diff, gathered, preferred_element_type=jnp.float32)
    grad_states = back(grad_embed)[0]
    return (grad_embed, grad_states)


def solution(mesh):
    in_specs = (
        P("dp", None, "mp"),
        P("mp"),
        P("mp", None),
        P("dp", None),
        P(("dp", "mp"), None, None),
        P(),
        P(),
        P(("dp", "mp"), None),
        P(("dp", "mp")),
    )
    out_specs = (P(("dp", "mp"), None), P(("dp", "mp"), None, None))
    return jax.shard_map(shards, mesh=mesh, in_specs=in_specs, out_specs=out_specs, check_vma=False)
```

profile of v0, /device:TPU:0, one launch (start us, length us, event | category | flops | bytes accessed | tf_op | source)
XLA Modules:
  0.0 156.2 jit_solution(10778247551571147130)
XLA Ops:
  7.2 0.0 copy-start
  7.2 0.0 copy-start.6
  7.2 0.0 all-reduce.2.cloned.1.call-start
  7.2 7.4 %fusion = f32[64,128]{1,0:T(8,128)S(1)} fusion(bf16[64,128,1024]{2,1,0:T(8,128)(2,1)} %param.9), kind=kLoop, calls=%fused_computation.2 | loop fusion | flops 25157632 | bytes 16809984 | tf_op jit(solution)/shard_map/reduce_sum | solution.py:41
  14.6 12.9 %psum.14 = f32[64,128]{1,0:T(8,128)S(1)} all-reduce(f32[64,128]{1,0:T(8,128)S(1)} %fusion), channel_id=1, replica_groups=mesh['dp'=8,'mp'=4] {'mp'}, use_global_device_ids=true, to_apply=%region_4.0 | all-reduce | flops 8192 | bytes 65536 | tf_op jit(solution)/shard_map/psum | solution.py:42
  27.6 0.0 copy-done.6
  27.6 0.0 copy-start.8
  27.6 0.0 copy-start.7
  27.6 0.0 copy-start.5
  27.6 7.6 %fusion.1 = f32[64,1024]{1,0:T(8,128)S(1)} fusion(bf16[64,128,1024]{2,1,0:T(8,128)(2,1)} %param.9, f32[64,128]{1,0:T(8,128)S(1)} %rsqrt_multiply_fusion), kind=kLoop, calls=%fused_computation.3 | loop fusion | flops 25100288 | bytes 17072128 | tf_op jit(solution)/shard_map/reduce_sum | solution.py:46
  35.3 0.0 copy-done
  35.3 0.0 copy-done.8
  35.3 1.2 fusion.31
  36.5 0.0 all-reduce.2.cloned.1.call-update
  36.5 0.0 all-gather.2.cloned.1.call-start
  36.6 32.7 %all-reduce.2.cloned.1.call-done = f32[64,1024]{1,0:T(8,128)} async-done(((f32[64,1024]{1,0:T(8,128)}), f32[64,1024]{1,0:T(8,128)}) %all-reduce.2.cloned.1.call-update) | async-done | bytes 262160 | tf_op jit(solution)/shard_map/psum | solution.py:49
  69.2 1.1 multiply_reduce_fusion.1
  70.3 1.7 %multiply_convert_fusion = bf16[64,1024]{1,0:T(8,128)(2,1)} fusion(f32[64,1024]{1,0:T(8,128)} %all-reduce.2.cloned.1.call-done, f32[64]{0:T(128)S(1)} %add_rsqrt_fusion), kind=kLoop, calls=%fused_computation.43 | loop fusion | flops 196608 | bytes 393472 | tf_op jit(solution)/shard_map/convert_element_type | solution.py:50
  72.0 0.0 all-gather.2.cloned.1.call-update
  72.1 0.0 copy-done.7
  72.1 0.1 mul.250
  72.2 0.0 copy-start.3
  72.2 2.7 %fusion.17 = f32[32,64]{1,0:T(8,128)S(1)} fusion(bf16[32,64,768]{2,1,0:T(8,128)(2,1)} %param.13), kind=kLoop, calls=%fused_computation.28 | loop fusion | flops 4716544 | bytes 3153920 | tf_op jit(solution)/shard_map/jvp()/reduce_sum | solution.py:19
  74.9 0.0 copy-done.5
  74.9 0.0 copy-start.9
  74.9 2.7 %fusion.19 = bf16[32,64,768]{2,1,0:T(8,128)(2,1)S(1)} fusion(bf16[32,64,768]{2,1,0:T(8,128)(2,1)} %param.13, f32[768]{0:T(1024)S(1)} %copy-done.5, f32[32,64]{1,0:T(8,128)S(1)} %fusion.40), kind=kLoop, calls=%fused_computation.30 | loop fusion | flops 6291456 | bytes 6302720 | tf_op jit(solution)/shard_map/jvp()/convert_element_type | solution.py:20
  77.6 0.0 copy-done.3
  77.6 7.7 %multiply_reduce_fusion = (f32[32,1024]{1,0:T(8,128)S(1)}, f32[2048,1024]{1,0:T(8,128)}) fusion(f32[32,64]{1,0:T(8,128)S(1)} %convert_element_type.45, bf16[2048,768]{1,0:T(8,128)(2,1)S(1)} %bitcast.31, bf16[768,1024]{1,0:T(8,128)(2,1)S(1)} %copy-done.3), kind=kOutput, calls=%fused_computation.25 | convolution fusion | flops 3242164224 | bytes 13246464 | tf_op jit(solution)/shard_map/jvp()/dot_general | solution.py:22
  85.3 0.1 multiply_reduce_fusion.3
  85.4 27.1 %all-gather.2.cloned.1.call-done = bf16[512,1024]{1,0:T(8,128)(2,1)} async-done(((bf16[64,1024]{1,0:T(8,128)(2,1)}), bf16[512,1024]{1,0:T(8,128)(2,1)}) %all-gather.2.cloned.1.call-update) | async-done | bytes 1048592 | tf_op jit(solution)/shard_map/all_gather | solution.py:51
  112.5 0.0 copy-done.9
  112.5 2.5 %fusion.45 = (f32[32]{0:T(128)S(1)}, f32[32,512]{1,0:T(8,128)S(1)}) fusion(bf16[512,1024]{1,0:T(8,128)(2,1)} %all-gather.2.cloned.1.call-done, s32[32]{0:T(128)S(1)} %copy-done.9), kind=kOutput, calls=%fused_computation.73 | convolution fusion | flops 67190752 | bytes 1114368 | tf_op jit(solution)/shard_map/dot_general | solution.py:59
  115.0 1.8 %fusion.46 = (f32[32]{0:T(128)S(1)}, f32[32,512]{1,0:T(8,128)S(1)}) fusion(bf16[512,1024]{1,0:T(8,128)(2,1)} %all-gather.2.cloned.1.call-done, f32[32,1024]{1,0:T(8,128)S(1)} %get-tuple-element.8, f32[32]{0:T(128)S(1)} %fusion.41), kind=kOutput, calls=%fused_computation.74 | convolution fusion | flops 33685472 | bytes 1245440 | tf_op jit(solution)/shard_map/dot_general | solution.py:60
  116.7 1.7 %multiply_reduce_fusion.2 = (f32[32]{0:T(128)S(1)}, f32[32,1024]{1,0:T(8,128)S(1)}) fusion(f32[32,1024]{1,0:T(8,128)S(1)} %get-tuple-element.8, bf16[512,1024]{1,0:T(8,128)(2,1)} %all-gather.2.cloned.1.call-done, f32[32,512]{1,0:T(8,128)S(1)} %get-tuple-element.11, f32[32,512]{1,0:T(8,128)S(1)} %get-tuple-element.13, f32[32]{0:T(128)S(1)} %get-tuple-element.10, ...), kind=kOutput, calls=%fused_computation.48 | convolution fusion | flops 33718240 | bytes 1442176 | tf_op jit(solution)/shard_map/dot_general | solution.py:66
  118.4 0.0 slice-start
  118.4 0.7 add_add_fusion.1
  119.1 0.0 slice-start.1
  119.1 0.0 copy-start.4
  119.1 11.1 %fusion.14 = (f32[2048,1024]{1,0:T(8,128)}, f32[2048,1024]{1,0:T(8,128)}) fusion(f32[2048,1024]{1,0:T(8,128)} %get-tuple-element.9, f32[2048]{0:T(1024)S(1)} %mul.250, f32[32,1024]{1,0:T(8,128)S(1)} %get-tuple-element.4), kind=kLoop, calls=%fused_computation.23 | loop fusion | flops 33554432 | bytes 25305088 | tf_op jit(solution)/shard_map/transpose(jvp())/mul | solution.py:22
  130.2 0.0 slice-done
  130.2 0.0 slice-done.1
  130.2 0.0 copy-done.4
  130.2 11.6 %fusion.24 = bf16[2048,768]{1,0:T(8,128)(2,1)} fusion(bf16[768,1024]{1,0:T(8,128)(2,1)S(1)} %copy-done.4, f32[2048,1024]{1,0:T(8,128)} %get-tuple-element.3, f32[2048,1024]{1,0:T(8,128)S(1)} %bitcast.29, f32[2048,1024]{1,0:T(8,128)} %get-tuple-element.2), kind=kOutput, calls=%fused_computation.36 | convolution fusion | flops 3233284096 | bytes 29884416 | tf_op jit(solution)/shard_map/transpose(jvp())/dot_general | solution.py:22
  141.9 0.0 copy-start.1
  141.9 0.0 copy-start.2
  141.9 4.1 %fusion.20 = f32[32,64]{1,0:T(8,128)S(1)} fusion(bf16[32,64,768]{2,1,0:T(8,128)(2,1)} %param.13, bf16[32,64,768]{2,1,0:T(8,128)(2,1)} %bitcast.30, f32[768]{0:T(1024)S(1)} %copy-done.5), kind=kLoop, calls=%fused_computation.31 | loop fusion | flops 7862272 | bytes 6302720 | tf_op jit(solution)/shard_map/transpose(jvp())/reduce_sum | solution.py:20
  146.0 0.0 copy-done.1
  146.0 0.6 copy-done.2
  146.6 2.8 %fusion.16 = bf16[32,64,768]{2,1,0:T(8,128)(2,1)} fusion(bf16[32,64,768]{2,1,0:T(8,128)(2,1)S(1)} %copy-done.1, f32[32,64]{1,0:T(8,128)S(1)} %multiply_multiply_fusion.3, f32[768]{0:T(1024)S(1)} %copy-done.5, f32[32,64]{1,0:T(8,128)S(1)} %fusion.40, bf16[2048,768]{1,0:T(8,128)(2,1)S(1)} %copy-done.2), kind=kLoop, calls=%fused_computation.27 | loop fusion | flops 12582912 | bytes 9456640 | tf_op jit(solution)/shard_map/transpose(jvp())/convert_element_type | solution.py:18
  (8 shorter events, 0.1 us)
Async XLA Ops:
  7.2 28.1 %copy-start = (bf16[1024,1024]{1,0:T(8,128)(2,1)S(1)}, bf16[1024,1024]{1,0:T(8,128)(2,1)}, u32[]{:S(2)}) copy-start(bf16[1024,1024]{1,0:T(8,128)(2,1)} %param.11) | copy-start | bytes 6291460
  7.2 20.4 %copy-start.6 = (s32[64,128]{1,0:T(8,128)S(1)}, s32[64,128]{1,0:T(8,128)}, u32[]{:S(2)}) copy-start(s32[64,128]{1,0:T(8,128)} %param.12) | copy-start | bytes 98308
  7.2 62.1 %all-reduce.2.cloned.1.call-start = ((), (), s32[]{:S(2)}) async-start(), calls=%async_computation | async-start | bytes 524288 | tf_op jit(solution)/shard_map/psum | solution.py:49
  27.6 7.7 %copy-start.8 = (f32[1024]{0:T(1024)S(1)}, f32[1024]{0:T(1024)}, u32[]{:S(2)}) copy-start(f32[1024]{0:T(1024)} %param.10) | copy-start | bytes 12292
  27.6 44.5 %copy-start.7 = (s32[32,64]{1,0:T(8,128)S(1)}, s32[32,64]{1,0:T(8,128)}, u32[]{:S(2)}) copy-start(s32[32,64]{1,0:T(8,128)} %param.16) | copy-start | bytes 24580
  27.6 47.2 %copy-start.5 = (f32[768]{0:T(1024)S(1)}, f32[768]{0:T(1024)}, u32[]{:S(2)}) copy-start(f32[768]{0:T(1024)} %param.14) | copy-start | bytes 9220
  36.5 76.0 %all-gather.2.cloned.1.call-start = ((), (), s32[]{:S(2)}) async-start(), calls=%async_computation.1 | async-start | bytes 1179648 | tf_op jit(solution)/shard_map/all_gather | solution.py:51
  72.2 5.4 %copy-start.3 = (bf16[768,1024]{1,0:T(8,128)(2,1)S(1)}, bf16[768,1024]{1,0:T(8,128)(2,1)}, u32[]{:S(2)}) copy-start(bf16[768,1024]{1,0:T(8,128)(2,1)} %param.15) | copy-start | bytes 4718596
  74.9 37.6 %copy-start.9 = (s32[32]{0:T(128)S(1)}, s32[32]{0:T(128)}, u32[]{:S(2)}) copy-start(s32[32]{0:T(128)} %param.17) | copy-start | bytes 388
  118.4 11.8 %slice-start = ((s8[8388608]{0:T(1024)(128)(4,1)}), s8[4194304]{0:T(1024)(128)(4,1)S(1)}, s32[]{:S(2)}) async-start(s8[8388608]{0:T(1024)(128)(4,1)} %bitcast.28), calls=%async_computation.2 | async-start | bytes 8388608
  119.1 11.1 %slice-start.1 = ((s8[8388608]{0:T(1024)(128)(4,1)}), s8[4194304]{0:T(1024)(128)(4,1)S(1)}, s32[]{:S(2)}) async-start(s8[8388608]{0:T(1024)(128)(4,1)} %bitcast.28), calls=%async_computation.3 | async-start | bytes 8388608
  119.1 11.1 %copy-start.4 = (bf16[768,1024]{1,0:T(8,128)(2,1)S(1)}, bf16[768,1024]{1,0:T(8,128)(2,1)}, u32[]{:S(2)}) copy-start(bf16[768,1024]{1,0:T(8,128)(2,1)} %param.15) | copy-start | bytes 4718596
  141.9 4.1 %copy-start.1 = (bf16[32,64,768]{2,1,0:T(8,128)(2,1)S(1)}, bf16[32,64,768]{2,1,0:T(8,128)(2,1)}, u32[]{:S(2)}) copy-start(bf16[32,64,768]{2,1,0:T(8,128)(2,1)} %param.13) | copy-start | bytes 9437188
  141.9 4.7 %copy-start.2 = (bf16[2048,768]{1,0:T(8,128)(2,1)S(1)}, bf16[2048,768]{1,0:T(8,128)(2,1)}, u32[]{:S(2)}) copy-start(bf16[2048,768]{1,0:T(8,128)(2,1)} %fusion.24) | copy-start | bytes 9437188
Sparse Core Ops, SparseCore 0:
  36.6 32.5 all-reduce.1
  72.2 40.2 all-gather.1
where the time goes:
time: 157 us; the launch traced here: 156 us
  waiting for transfers between devices  59.8 us (38%)
  other arithmetic  41.9 us (27%)
  matrix products  26.5 us (17%)
  between operations  14.2 us (9%)
  blocking collectives  12.9 us (8%)
    psum x1, waiting for transfers between devices, shards(): summed = lax.psum(partial_embed, 'mp')  32.7 us
    all_gather x1, waiting for transfers between devices, shards(): gathered = lax.all_gather(group_emb, 'dp', axis=0, tiled=True)  27.1 us
    dot_general x2, matrix products, student_forward(): jnp.dot(flat, proj, preferred_element_type=jnp.float32)  19.3 us
    psum x1, blocking collectives, shards(): squares = lax.psum(partial_squares, 'mp')  12.9 us
    mul x1, other arithmetic, student_forward(): jax.nn.gelu(jnp.dot(flat, proj, preferred_element_type=jnp.float32), appr...  11.1 us
    reduce_sum x1, other arithmetic, shards(): pooled = jnp.sum(values * weight[:, :, None], axis=1)  7.65 us
    reduce_sum x1, other arithmetic, shards(): partial_squares = jnp.sum(values * values, axis=-1)  7.38 us
    reduce_sum x1, other arithmetic, student_forward(): normed = (values * scale * gain).astype(jnp.bfloat16)  4.07 us
  transfers between devices with their start and end apart: 2, of which 2 were waited for; matrix products, arithmetic and copies ran while one was open for 8% of the time, Pallas kernels for 0%

commit v1 on v0

--- a/solution.py
+++ b/solution.py
@@ -4,6 +4,17 @@
 from jax.sharding import PartitionSpec as P
 
 D = 4096
+
+
+def turned_line(x, mesh_axis, dim):
+    peers = lax.axis_size(mesh_axis)
+    right = [(i, (i + 1) % peers) for i in range(peers)]
+    pieces = [x]
+    for reach in range(1, peers):
+        pieces = [lax.ppermute(pieces[0], mesh_axis, right), *pieces]
+    out = jnp.concatenate(pieces, axis=dim)
+    shift = (lax.axis_index(mesh_axis) + 1) * pieces[-1].shape[dim]
+    return jnp.roll(out, shift, axis=dim)
 
 
 def unit_rows(values):
@@ -48,7 +59,7 @@
     partial_embed = jnp.dot(tpooled, teacher_proj, preferred_element_type=jnp.float32)
     summed = lax.psum(partial_embed, "mp")
     group_emb = unit_rows(summed).astype(jnp.bfloat16)
-    gathered = lax.all_gather(group_emb, "dp", axis=0, tiled=True)
+    gathered = turned_line(group_emb, "dp", 0)
     semb, back = jax.vjp(
         lambda st: student_forward(st, student_gain, student_proj, student_mask), student_states
     )

time: 157 us -> 188 us (1.20)
  waiting for transfers between devices: 59.8 us -> 76.3 us
  local copies, waits for them, and re-layouts: 0.73 us -> 10 us
  other arithmetic: 41.9 us -> 44.3 us
    ppermute x0 -> x7, waiting for transfers between devices: none -> 43.6 us  [turned_line(): pieces = [lax.ppermute(pieces[0], mesh_axis, right), *pieces]]
    all_gather x1 -> x0, waiting for transfers between devices: 27.1 us -> none  [shards(): gathered = lax.all_gather(group_emb, 'dp', axis=0, tiled=True)]
    unnamed x24 -> x38, local copies, waits for them, and re-layouts: 0.66 us -> 9.95 us
  transfers between devices with their start and end apart: 2 -> 8, of which waited for: 2 -> 7; matrix products, arithmetic and copies ran while one was open for 8% -> 9% of each run, Pallas kernels for 0% -> 0%
where the time goes in v1:
time: 188 us
  waiting for transfers between devices  76.3 us (41%)
  other arithmetic  44.3 us (24%)
  matrix products  28 us (15%)
  between operations  14.2 us (8%)
  blocking collectives  12.9 us (7%)
  local copies, waits for them, and re-layouts  10 us (5%)
    ppermute x7, waiting for transfers between devices, turned_line(): pieces = [lax.ppermute(pieces[0], mesh_axis, right), *pieces]  43.6 us
    psum x1, waiting for transfers between devices, shards(): summed = lax.psum(partial_embed, 'mp')  32.7 us
    dot_general x2, matrix products, student_forward(): jnp.dot(flat, proj, preferred_element_type=jnp.float32)  21 us
    psum x1, blocking collectives, shards(): squares = lax.psum(partial_squares, 'mp')  12.9 us
    mul x1, other arithmetic, student_forward(): jax.nn.gelu(jnp.dot(flat, proj, preferred_element_type=jnp.float32), appr...  11.1 us
    unnamed x38, local copies, waits for them, and re-layouts  9.95 us
    reduce_sum x1, other arithmetic, shards(): pooled = jnp.sum(values * weight[:, :, None], axis=1)  7.65 us
    reduce_sum x1, other arithmetic, shards(): partial_squares = jnp.sum(values * values, axis=-1)  7.38 us
  transfers between devices with their start and end apart: 8, of which 7 were waited for; matrix products, arithmetic and copies ran while one was open for 9% of the time, Pallas kernels for 0%

profile of v1, /device:TPU:0, one launch (start us, length us, event | category | flops | bytes accessed | tf_op | source)
XLA Modules:
  0.0 187.6 jit_solution(16814727736731190001)
XLA Ops:
  7.2 0.0 copy-start
  7.2 0.0 copy-start.6
  7.2 0.0 all-reduce.2.cloned.1.call-start
  7.2 7.4 %fusion = f32[64,128]{1,0:T(8,128)S(1)} fusion(bf16[64,128,1024]{2,1,0:T(8,128)(2,1)} %param.9), kind=kLoop, calls=%fused_computation.2 | loop fusion | flops 25157632 | bytes 16809984 | tf_op jit(solution)/shard_map/reduce_sum | solution.py:52
  14.6 12.9 %psum.14 = f32[64,128]{1,0:T(8,128)S(1)} all-reduce(f32[64,128]{1,0:T(8,128)S(1)} %fusion), channel_id=1, replica_groups=mesh['dp'=8,'mp'=4] {'mp'}, use_global_device_ids=true, to_apply=%region_4.0 | all-reduce | flops 8192 | bytes 65536 | tf_op jit(solution)/shard_map/psum | solution.py:53
  27.6 0.0 copy-done.6
  27.6 0.0 copy-start.8
  27.6 7.6 %fusion.1 = f32[64,1024]{1,0:T(8,128)S(1)} fusion(bf16[64,128,1024]{2,1,0:T(8,128)(2,1)} %param.9, f32[64,128]{1,0:T(8,128)S(1)} %rsqrt_multiply_fusion), kind=kLoop, calls=%fused_computation.3 | loop fusion | flops 25100288 | bytes 17072128 | tf_op jit(solution)/shard_map/reduce_sum | solution.py:57
  35.3 0.0 copy-done
  35.3 0.0 copy-done.8
  35.3 0.0 copy-start.5
  35.3 0.0 copy-start.7
  35.3 1.2 fusion.36
  36.5 0.0 all-reduce.2.cloned.1.call-update
  36.5 32.7 %all-reduce.2.cloned.1.call-done = f32[64,1024]{1,0:T(8,128)} async-done(((f32[64,1024]{1,0:T(8,128)}), f32[64,1024]{1,0:T(8,128)}) %all-reduce.2.cloned.1.call-update) | async-done | bytes 262160 | tf_op jit(solution)/shard_map/psum | solution.py:60
  69.2 1.1 multiply_reduce_fusion.1
  70.3 1.0 multiply_convert_fusion
  71.4 1.5 collective-permute-start
  72.9 6.2 %collective-permute-done = bf16[64,1024]{1,0:T(8,128)(2,1)S(1)} collective-permute-done((bf16[64,1024]{1,0:T(8,128)(2,1)S(1)}, bf16[64,1024]{1,0:T(8,128)(2,1)S(1)}, u32[]{:S(2)}, u32[]{:S(2)}) %collective-permute-start) | collective-permute-done | bytes 131104 | tf_op jit(solution)/shard_map/ppermute | solution.py:14
  79.1 0.0 collective-permute-start.1
  79.1 7.7 %collective-permute-done.1 = bf16[64,1024]{1,0:T(8,128)(2,1)S(1)} collective-permute-done((bf16[64,1024]{1,0:T(8,128)(2,1)S(1)}, bf16[64,1024]{1,0:T(8,128)(2,1)S(1)}, u32[]{:S(2)}, u32[]{:S(2)}) %collective-permute-start.1) | collective-permute-done | bytes 131104 | tf_op jit(solution)/shard_map/ppermute | solution.py:14
  86.8 0.0 collective-permute-start.2
  86.8 7.7 %collective-permute-done.2 = bf16[64,1024]{1,0:T(8,128)(2,1)S(1)} collective-permute-done((bf16[64,1024]{1,0:T(8,128)(2,1)S(1)}, bf16[64,1024]{1,0:T(8,128)(2,1)S(1)}, u32[]{:S(2)}, u32[]{:S(2)}) %collective-permute-start.2) | collective-permute-done | bytes 131104 | tf_op jit(solution)/shard_map/ppermute | solution.py:14
  94.4 0.0 collective-permute-start.3
  94.4 2.6 %fusion.17 = f32[32,64]{1,0:T(8,128)S(1)} fusion(bf16[32,64,768]{2,1,0:T(8,128)(2,1)} %param.13), kind=kLoop, calls=%fused_computation.28 | loop fusion | flops 4716544 | bytes 3153920 | tf_op jit(solution)/shard_map/jvp()/reduce_sum | solution.py:30
  97.0 5.9 %collective-permute-done.3 = bf16[64,1024]{1,0:T(8,128)(2,1)S(1)} collective-permute-done((bf16[64,1024]{1,0:T(8,128)(2,1)S(1)}, bf16[64,1024]{1,0:T(8,128)(2,1)S(1)}, u32[]{:S(2)}, u32[]{:S(2)}) %collective-permute-start.3) | collective-permute-done | bytes 131104 | tf_op jit(solution)/shard_map/ppermute | solution.py:14
  102.9 0.0 collective-permute-start.4
  103.0 8.5 %collective-permute-done.4 = bf16[64,1024]{1,0:T(8,128)(2,1)S(1)} collective-permute-done((bf16[64,1024]{1,0:T(8,128)(2,1)S(1)}, bf16[64,1024]{1,0:T(8,128)(2,1)S(1)}, u32[]{:S(2)}, u32[]{:S(2)}) %collective-permute-start.4) | collective-permute-done | bytes 131104 | tf_op jit(solution)/shard_map/ppermute | solution.py:14
  111.4 0.0 collective-permute-start.5
  111.4 4.3 %fusion.19 = bf16[32,64,768]{2,1,0:T(8,128)(2,1)} fusion(bf16[32,64,768]{2,1,0:T(8,128)(2,1)} %param.13, f32[768]{0:T(1024)S(1)} %copy-done.5, f32[32,64]{1,0:T(8,128)S(1)} %fusion.44), kind=kLoop, calls=%fused_computation.30 | loop fusion | flops 6291456 | bytes 6302720 | tf_op jit(solution)/shard_map/jvp()/convert_element_type | solution.py:31
  115.8 0.0 copy-done.7
  115.8 0.1 mul.254
  115.8 9.4 %multiply_reduce_fusion = (f32[32,1024]{1,0:T(8,128)S(1)}, f32[2048,1024]{1,0:T(8,128)}) fusion(f32[32,64]{1,0:T(8,128)S(1)} %convert_element_type.45, bf16[2048,768]{1,0:T(8,128)(2,1)} %bitcast.27, bf16[768,1024]{1,0:T(8,128)(2,1)} %param.15), kind=kOutput, calls=%fused_computation.25 | convolution fusion | flops 3242164224 | bytes 13246464 | tf_op jit(solution)/shard_map/jvp()/dot_general | solution.py:33
  125.2 0.1 multiply_reduce_fusion.3
  125.4 0.0 collective-permute-done.5
  125.4 0.2 collective-permute-start.6
  125.6 7.6 %collective-permute-done.6 = bf16[64,1024]{1,0:T(8,128)(2,1)S(1)} collective-permute-done((bf16[64,1024]{1,0:T(8,128)(2,1)S(1)}, bf16[64,1024]{1,0:T(8,128)(2,1)S(1)}, u32[]{:S(2)}, u32[]{:S(2)}) %collective-permute-start.6) | collective-permute-done | bytes 131104 | tf_op jit(solution)/shard_map/ppermute | solution.py:14
  133.3 0.7 constant_dynamic-update-slice_fusion.15
  133.9 0.7 constant_dynamic-update-slice_fusion.14
  134.6 0.7 constant_dynamic-update-slice_fusion.13
  135.3 0.7 constant_dynamic-update-slice_fusion.12
  135.9 0.7 constant_dynamic-update-slice_fusion.11
  136.6 0.7 constant_dynamic-update-slice_fusion.10
  137.2 0.7 constant_dynamic-update-slice_fusion.9
  137.9 0.7 constant_dynamic-update-slice_fusion.8
  138.7 0.7 constant_dynamic-update-slice_fusion.7
  139.3 0.7 constant_dynamic-update-slice_fusion.6
  140.0 0.7 constant_dynamic-update-slice_fusion.5
  140.7 0.7 constant_dynamic-update-slice_fusion.4
  141.3 0.7 constant_dynamic-update-slice_fusion.3
  142.0 0.7 constant_dynamic-update-slice_fusion.2
  142.6 0.7 constant_dynamic-update-slice_fusion.1
  143.3 0.7 constant_dynamic-update-slice_fusion
  144.1 2.3 %fusion.53 = (f32[32]{0:T(128)S(1)}, f32[32,512]{1,0:T(8,128)S(1)}) fusion(bf16[1024,1024]{1,0:T(8,128)(2,1)} %constant_dynamic-update-slice_fusion, s32[]{:T(128)S(6)} %select_n.14, s32[32]{0:T(128)S(1)} %copy-done.9), kind=kOutput, calls=%fused_computation.95 | convolution fusion | flops 67190752 | bytes 2163968 | tf_op jit(solution)/shard_map/dot_general | solution.py:70
  146.3 1.8 fusion.56
  148.1 1.7 multiply_reduce_fusion.2
  149.8 0.0 slice-start
  149.8 0.7 add_add_fusion.1
  150.5 11.1 %fusion.14 = (f32[2048,1024]{1,0:T(8,128)}, f32[2048,1024]{1,0:T(8,128)}) fusion(f32[2048,1024]{1,0:T(8,128)} %get-tuple-element.9, f32[2048]{0:T(1024)S(1)} %mul.254, f32[32,1024]{1,0:T(8,128)S(1)} %get-tuple-element.4), kind=kLoop, calls=%fused_computation.23 | loop fusion | flops 33554432 | bytes 25305088 | tf_op jit(solution)/shard_map/transpose(jvp())/mul | solution.py:33
  161.6 0.0 slice-done
  161.6 11.6 %fusion.24 = bf16[2048,768]{1,0:T(8,128)(2,1)} fusion(bf16[768,1024]{1,0:T(8,128)(2,1)S(1)} %copy-done.3, f32[2048,1024]{1,0:T(8,128)} %get-tuple-element.3, f32[2048,1024]{1,0:T(8,128)S(1)} %bitcast.25, f32[2048,1024]{1,0:T(8,128)} %get-tuple-element.2), kind=kOutput, calls=%fused_computation.36 | convolution fusion | flops 3233284096 | bytes 29884416 | tf_op jit(solution)/shard_map/transpose(jvp())/dot_general | solution.py:33
  173.3 4.1 %fusion.20 = f32[32,64]{1,0:T(8,128)S(1)} fusion(bf16[32,64,768]{2,1,0:T(8,128)(2,1)} %param.13, bf16[32,64,768]{2,1,0:T(8,128)(2,1)} %bitcast.26, f32[768]{0:T(1024)S(1)} %copy-done.5), kind=kLoop, calls=%fused_computation.31 | loop fusion | flops 7862272 | bytes 6302720 | tf_op jit(solution)/shard_map/transpose(jvp())/reduce_sum | solution.py:31
  177.3 0.6 copy-done.2
  177.9 2.8 %fusion.16 = bf16[32,64,768]{2,1,0:T(8,128)(2,1)} fusion(bf16[32,64,768]{2,1,0:T(8,128)(2,1)S(1)} %copy-done.1, f32[32,64]{1,0:T(8,128)S(1)} %multiply_multiply_fusion.3, f32[768]{0:T(1024)S(1)} %copy-done.5, f32[32,64]{1,0:T(8,128)S(1)} %fusion.44, bf16[2048,768]{1,0:T(8,128)(2,1)S(1)} %copy-done.2), kind=kLoop, calls=%fused_computation.27 | loop fusion | flops 12582912 | bytes 9456640 | tf_op jit(solution)/shard_map/transpose(jvp())/convert_element_type | solution.py:29
  (20 shorter events, 0.1 us)
Async XLA Ops:
  7.2 28.1 %copy-start = (bf16[1024,1024]{1,0:T(8,128)(2,1)S(1)}, bf16[1024,1024]{1,0:T(8,128)(2,1)}, u32[]{:S(2)}) copy-start(bf16[1024,1024]{1,0:T(8,128)(2,1)} %param.11) | copy-start | bytes 6291460
  7.2 20.4 %copy-start.6 = (s32[64,128]{1,0:T(8,128)S(1)}, s32[64,128]{1,0:T(8,128)}, u32[]{:S(2)}) copy-start(s32[64,128]{1,0:T(8,128)} %param.12) | copy-start | bytes 98308
  7.2 62.1 %all-reduce.2.cloned.1.call-start = ((), (), s32[]{:S(2)}) async-start(), calls=%async_computation | async-start | bytes 524288 | tf_op jit(solution)/shard_map/psum | solution.py:60
  27.6 7.7 %copy-start.8 = (f32[1024]{0:T(1024)S(1)}, f32[1024]{0:T(1024)}, u32[]{:S(2)}) copy-start(f32[1024]{0:T(1024)} %param.10) | copy-start | bytes 12292
  35.3 76.2 %copy-start.5 = (f32[768]{0:T(1024)S(1)}, f32[768]{0:T(1024)}, u32[]{:S(2)}) copy-start(f32[768]{0:T(1024)} %param.14) | copy-start | bytes 9220
  35.3 80.5 %copy-start.7 = (s32[32,64]{1,0:T(8,128)S(1)}, s32[32,64]{1,0:T(8,128)}, u32[]{:S(2)}) copy-start(s32[32,64]{1,0:T(8,128)} %param.16) | copy-start | bytes 24580
  71.4 7.7 %collective-permute-start = (bf16[64,1024]{1,0:T(8,128)(2,1)S(1)}, bf16[64,1024]{1,0:T(8,128)(2,1)S(1)}, u32[]{:S(2)}, u32[]{:S(2)}) collective-permute-start(bf16[64,1024]{1,0:T(8,128)(2,1)S(1)} %multiply_convert_fusion), channel_id=1, source_target_pairs={{0,4},{4,8},{8,12},{12,16},{16,20},{20,24},{24,28},{28,0},{1,5},{5... | collective-permute-start | bytes 393224 | tf_op jit(solution)/shard_map/ppermute | solution.py:14
  79.1 7.7 %collective-permute-start.1 = (bf16[64,1024]{1,0:T(8,128)(2,1)S(1)}, bf16[64,1024]{1,0:T(8,128)(2,1)S(1)}, u32[]{:S(2)}, u32[]{:S(2)}) collective-permute-start(bf16[64,1024]{1,0:T(8,128)(2,1)S(1)} %collective-permute-done), channel_id=1, source_target_pairs={{0,4},{4,8},{8,12},{12,16},{16,20},{20,24},{24,28},{28,0},{1,5},{5... | collective-permute-start | bytes 393224 | tf_op jit(solution)/shard_map/ppermute | solution.py:14
  86.8 7.7 %collective-permute-start.2 = (bf16[64,1024]{1,0:T(8,128)(2,1)S(1)}, bf16[64,1024]{1,0:T(8,128)(2,1)S(1)}, u32[]{:S(2)}, u32[]{:S(2)}) collective-permute-start(bf16[64,1024]{1,0:T(8,128)(2,1)S(1)} %collective-permute-done.1), channel_id=1, source_target_pairs={{0,4},{4,8},{8,12},{12,16},{16,20},{20,24},{24,28},{28,0},{1,5},{5... | collective-permute-start | bytes 393224 | tf_op jit(solution)/shard_map/ppermute | solution.py:14
  94.4 8.5 %collective-permute-start.3 = (bf16[64,1024]{1,0:T(8,128)(2,1)S(1)}, bf16[64,1024]{1,0:T(8,128)(2,1)S(1)}, u32[]{:S(2)}, u32[]{:S(2)}) collective-permute-start(bf16[64,1024]{1,0:T(8,128)(2,1)S(1)} %collective-permute-done.2), channel_id=1, source_target_pairs={{0,4},{4,8},{8,12},{12,16},{16,20},{20,24},{24,28},{28,0},{1,5},{5... | collective-permute-start | bytes 393224 | tf_op jit(solution)/shard_map/ppermute | solution.py:14
  102.9 8.5 %collective-permute-start.4 = (bf16[64,1024]{1,0:T(8,128)(2,1)S(1)}, bf16[64,1024]{1,0:T(8,128)(2,1)S(1)}, u32[]{:S(2)}, u32[]{:S(2)}) collective-permute-start(bf16[64,1024]{1,0:T(8,128)(2,1)S(1)} %collective-permute-done.3), channel_id=1, source_target_pairs={{0,4},{4,8},{8,12},{12,16},{16,20},{20,24},{24,28},{28,0},{1,5},{5... | collective-permute-start | bytes 393224 | tf_op jit(solution)/shard_map/ppermute | solution.py:14
  111.4 13.9 %collective-permute-start.5 = (bf16[64,1024]{1,0:T(8,128)(2,1)S(1)}, bf16[64,1024]{1,0:T(8,128)(2,1)S(1)}, u32[]{:S(2)}, u32[]{:S(2)}) collective-permute-start(bf16[64,1024]{1,0:T(8,128)(2,1)S(1)} %collective-permute-done.4), channel_id=1, source_target_pairs={{0,4},{4,8},{8,12},{12,16},{16,20},{20,24},{24,28},{28,0},{1,5},{5... | collective-permute-start | bytes 393224 | tf_op jit(solution)/shard_map/ppermute | solution.py:14
  115.8 22.1 %copy-start.4 = (f32[64,1024]{1,0:T(8,128)S(1)}, f32[64,1024]{1,0:T(8,128)}, u32[]{:S(2)}) copy-start(f32[64,1024]{1,0:T(8,128)} %all-reduce.2.cloned.1.call-done) | copy-start | bytes 786436
  115.8 28.2 %copy-start.9 = (s32[32]{0:T(128)S(1)}, s32[32]{0:T(128)}, u32[]{:S(2)}) copy-start(s32[32]{0:T(128)} %param.17) | copy-start | bytes 388
  125.4 7.9 %collective-permute-start.6 = (bf16[64,1024]{1,0:T(8,128)(2,1)S(1)}, bf16[64,1024]{1,0:T(8,128)(2,1)S(1)}, u32[]{:S(2)}, u32[]{:S(2)}) collective-permute-start(bf16[64,1024]{1,0:T(8,128)(2,1)S(1)} %collective-permute-done.5), channel_id=1, source_target_pairs={{0,4},{4,8},{8,12},{12,16},{16,20},{20,24},{24,28},{28,0},{1,5},{5... | collective-permute-start | bytes 393224 | tf_op jit(solution)/shard_map/ppermute | solution.py:14
  149.8 11.8 %slice-start = ((s8[8388608]{0:T(1024)(128)(4,1)}), s8[4194304]{0:T(1024)(128)(4,1)S(1)}, s32[]{:S(2)}) async-start(s8[8388608]{0:T(1024)(128)(4,1)} %bitcast.24), calls=%async_computation.1 | async-start | bytes 8388608
  150.5 11.1 %slice-start.1 = ((s8[8388608]{0:T(1024)(128)(4,1)}), s8[4194304]{0:T(1024)(128)(4,1)S(1)}, s32[]{:S(2)}) async-start(s8[8388608]{0:T(1024)(128)(4,1)} %bitcast.24), calls=%async_computation.2 | async-start | bytes 8388608
  150.5 11.1 %copy-start.3 = (bf16[768,1024]{1,0:T(8,128)(2,1)S(1)}, bf16[768,1024]{1,0:T(8,128)(2,1)}, u32[]{:S(2)}) copy-start(bf16[768,1024]{1,0:T(8,128)(2,1)} %param.15) | copy-start | bytes 4718596
  173.2 4.1 %copy-start.1 = (bf16[32,64,768]{2,1,0:T(8,128)(2,1)S(1)}, bf16[32,64,768]{2,1,0:T(8,128)(2,1)}, u32[]{:S(2)}) copy-start(bf16[32,64,768]{2,1,0:T(8,128)(2,1)} %param.13) | copy-start | bytes 9437188
  173.2 4.7 %copy-start.2 = (bf16[2048,768]{1,0:T(8,128)(2,1)S(1)}, bf16[2048,768]{1,0:T(8,128)(2,1)}, u32[]{:S(2)}) copy-start(bf16[2048,768]{1,0:T(8,128)(2,1)} %fusion.24) | copy-start | bytes 9437188
Sparse Core Ops, SparseCore 0:
  36.6 32.5 all-reduce.1
